TPU v7x, 8 devices: a whole 2x2x1 slice. The times are simulated.
8 devices in a mesh: tp: 4 (over z, y, x), dp: 2 (over core).
Axes of the slice: x: 2, y: 2, z: 1, core: 2. Of those that a mesh axis runs over, the one named last changes fastest.
Arguments:
- x: bfloat16 [512, 2048], P('dp')
- lengths: int32 [512], P('dp')
- cache: bfloat16 [2, 512, 512, 576], P(None, 'dp')
- attn_norm: bfloat16 [2, 2048], replicated
- ffn_norm: bfloat16 [2, 2048], replicated
- wq: bfloat16 [2, 2048, 9216], P(None, None, 'tp')
- wo: bfloat16 [2, 8192, 2048], P(None, 'tp')
- w1: bfloat16 [2, 2048, 11264], P(None, None, ('dp', 'tp'))
- w3: bfloat16 [2, 2048, 11264], P(None, None, ('dp', 'tp'))
- w2: bfloat16 [2, 11264, 2048], P(None, ('dp', 'tp'))
Outputs:
- output: bfloat16 [512, 2048], P('dp')
All inputs are finite; a program needn't handle non-finite values.
Results may differ from a plain program's by a relative error of at most 0.02.
Values are sent between devices in bfloat16 or wider.
A program may use at most 1.5 GiB of HBM per device.

v0:
```python
import jax
import jax.numpy as jnp
from jax import lax
from jax.sharding import PartitionSpec as P

LAT = 512
EPS = 1e-6
SCALE = 192 ** -0.5


def _rmsnorm(v, w):
    vf = v.astype(jnp.float32)
    r = lax.rsqrt(jnp.mean(vf * vf, axis=-1, keepdims=True) + EPS)
    return (vf * r * w.astype(jnp.float32)).astype(jnp.bfloat16)


def solution(mesh):
    def body(x, lengths, cache, attn_norm, ffn_norm, wq, wo, w1, w3, w2):
        nb = x.shape[0]
        n_layers, _, s_len, kv = cache.shape
        nh = wq.shape[2] // kv
        keep = (jnp.arange(s_len)[None, :] < lengths[:, None])[:, None, :]
        for l in range(n_layers):
            c = cache[l]
            h = _rmsnorm(x, attn_norm[l])
            q = jnp.dot(h, wq[l], preferred_element_type=jnp.float32).astype(jnp.bfloat16).reshape(nb, nh, kv)
            s = jnp.einsum('bhk,btk->bht', q, c, preferred_element_type=jnp.float32) * SCALE
            p = jax.nn.softmax(jnp.where(keep, s, -jnp.inf), axis=-1).astype(jnp.bfloat16)
            o = jnp.einsum('bht,btk->bhk', p, c[:, :, :LAT], preferred_element_type=jnp.float32)
            o = o.astype(jnp.bfloat16).reshape(nb, nh * LAT)
            attn = lax.psum(jnp.dot(o, wo[l], preferred_element_type=jnp.float32), 'tp')
            x = x + attn.astype(jnp.bfloat16)
            g = _rmsnorm(x, ffn_norm[l])
            gg = lax.all_gather(g, 'dp', axis=0, tiled=True)
            u = jnp.dot(gg, w3[l], preferred_element_type=jnp.float32)
            v = jnp.dot(gg, w1[l], preferred_element_type=jnp.float32)
            a = (jax.nn.silu(u) * v).astype(jnp.bfloat16)
            yp = jnp.dot(a, w2[l], preferred_element_type=jnp.float32)
            y = lax.psum_scatter(yp, 'dp', scatter_dimension=0, tiled=True)
            y = lax.psum(y, 'tp')
            x = x + y.astype(jnp.bfloat16)
        return x

    in_specs = (
        P('dp', None),
        P('dp'),
        P(None, 'dp', None, None),
        P(None, None),
        P(None, None),
        P(None, None, 'tp'),
        P(None, 'tp', None),
        P(None, None, ('dp', 'tp')),
        P(None, None, ('dp', 'tp')),
        P(None, ('dp', 'tp'), None),
    )
    return jax.shard_map(body, mesh=mesh, in_specs=in_specs, out_specs=P('dp', None), check_vma=False)
```

profile of v0, /device:TPU:0, one launch (start us, length us, event | category | flops | bytes accessed | tf_op | source)
XLA Modules:
  0.0 834.2 jit_solution(10832799005805966741)
XLA Ops:
  6.5 0.0 all-gather.3.cloned.1.call-start
  6.5 1.4 slice_convert_fusion.1
  7.9 1.5 fusion.54
  9.4 6.7 fusion.36
  16.1 0.0 copy-start.7
  16.1 0.6 copy.13
  16.8 2.2 copy.14
  19.0 0.0 copy-done.7
  19.0 0.8 iota_compare_fusion
  19.8 0.0 copy-start
  19.8 0.0 copy-start.4
  19.8 194.7 %slice_bitcast_fusion = (bf16[256,512,576]{1,2,0:T(8,128)(2,1)}, bf16[256,512,576]{1,2,0:T(8,128)(2,1)}) fusion(bf16[2,256,512,576]{2,3,1,0:T(8,128)(2,1)} %param.12), kind=kLoop, calls=%fused_computation.2 | loop fusion | bytes 603979776 | tf_op jit(solution)/shard_map/squeeze | solution.py:24
  214.5 0.0 copy-done
  214.5 0.0 copy-done.4
  214.5 47.7 %multiply_select_fusion.1 = f32[256,4,512]{2,1,0:T(4,128)S(1)} fusion(bf16[256,4,576]{2,1,0:T(4,128)(2,1)S(1)} %copy-done, pred[256,512]{1,0:T(8,128)(4,1)S(1)} %copy-done.4, bf16[2,256,512,576]{2,3,1,0:T(8,128)(2,1)} %param.12), kind=kOutput, calls=%fused_computation.67 | convolution fusion | flops 605028352 | bytes 154402816 | tf_op jit(solution)/shard_map/bhk,btk->bht/dot_general | solution.py:27
  262.2 2.3 fusion.86
  264.5 47.8 %fusion.66 = bf16[256,4,512]{2,1,0:T(4,128)(2,1)S(1)} fusion(bf16[256,512,576]{1,2,0:T(8,128)(2,1)} %get-tuple-element.12, f32[256,4,512]{2,1,0:T(4,128)} %get-tuple-element.18, f32[256,4]{1,0:T(8,128)S(1)} %get-tuple-element.17), kind=kOutput, calls=%fused_computation.70 | convolution fusion | flops 538443776 | bytes 137367552 | tf_op jit(solution)/shard_map/bht,btk->bhk/dot_general | solution.py:29
  312.3 0.3 copy.21
  312.6 7.1 fusion.14
  319.7 0.0 copy-start.1
  319.7 77.8 %all-reduce.4 = bf16[256,2048]{1,0:T(8,128)(2,1)S(1)} all-reduce(f32[256,2048]{1,0:T(8,128)} %fusion.14), channel_id=1, replica_groups=mesh['tp'=4,'dp'=2] {'tp'}, use_global_device_ids=true, to_apply=%region_3.4 | all-reduce | flops 524288 | bytes 3145728 | tf_op jit(solution)/shard_map/psum | solution.py:31
  397.5 0.0 copy-done.1
  397.5 0.0 copy-start.5
  397.5 0.5 fusion.57
  398.1 0.2 copy-done.5
  398.3 1.3 fusion.59
  399.5 0.0 all-gather.3.cloned.1.call-update
  399.6 0.0 reduce-scatter.3.cloned.1.call-start
  399.6 8.2 all-gather.3.cloned.1.call-done
  407.8 0.0 copy-start.8
  407.8 8.4 %fusion.28 = f32[512,1408]{1,0:T(8,128)} fusion(bf16[512,2048]{1,0:T(8,128)(2,1)} %all-gather.3.cloned.1.call-done, bf16[2,2048,1408]{2,1,0:T(8,128)(2,1)} %param.18), kind=kOutput, calls=%fused_computation.30 | convolution fusion | flops 2952790016 | bytes 10747904 | tf_op jit(solution)/shard_map/dot_general | solution.py:35
  416.2 0.0 copy-done.8
  416.3 13.8 %fusion.24 = f32[512,2048]{1,0:T(8,128)} fusion(bf16[2,1408,2048]{2,1,0:T(8,128)(2,1)} %param.19, bf16[512,2048]{1,0:T(8,128)(2,1)S(1)} %copy-done.8, bf16[2,2048,1408]{2,1,0:T(8,128)(2,1)} %param.17, f32[512,1408]{1,0:T(8,128)} %fusion.28), kind=kOutput, calls=%fused_computation.26 | convolution fusion | flops 5909905408 | bytes 20709376 | tf_op jit(solution)/shard_map/dot_general | solution.py:38
  430.1 0.0 reduce-scatter.3.cloned.1.call-update
  430.1 0.0 all-gather.5.cloned.1.call-start
  430.1 10.0 %reduce-scatter.3.cloned.1.call-done = f32[256,2048]{1,0:T(8,128)} async-done(((f32[512,2048]{1,0:T(8,128)}), f32[256,2048]{1,0:T(8,128)}) %reduce-scatter.3.cloned.1.call-update) | async-done | bytes 2097168 | tf_op jit(solution)/shard_map/reduce_scatter | solution.py:39
  440.2 77.3 %all-reduce.5 = bf16[256,2048]{1,0:T(8,128)(2,1)S(1)} all-reduce(f32[256,2048]{1,0:T(8,128)} %reduce-scatter.3.cloned.1.call-done), channel_id=1, replica_groups=mesh['tp'=4,'dp'=2] {'tp'}, use_global_device_ids=true, to_apply=%region_6.7 | all-reduce | flops 524288 | bytes 3145728 | tf_op jit(solution)/shard_map/psum | solution.py:40
  517.5 0.0 copy-start.6
  517.5 0.5 fusion.60
  518.0 0.0 copy-start.2
  518.1 1.0 copy-done.2
  519.0 0.0 copy-done.6
  519.0 6.4 fusion.39
  525.4 0.6 copy.16
  526.0 1.4 copy.17
  527.4 47.7 %multiply_select_fusion = f32[256,4,512]{2,1,0:T(4,128)S(1)} fusion(bf16[256,4,576]{2,1,0:T(4,128)(2,1)S(1)} %copy.17, pred[256,512]{1,0:T(8,128)(4,1)S(1)} %copy-done.4, bf16[2,256,512,576]{2,3,1,0:T(8,128)(2,1)} %param.12), kind=kOutput, calls=%fused_computation.65 | convolution fusion | flops 605028352 | bytes 154402816 | tf_op jit(solution)/shard_map/bhk,btk->bht/dot_general | solution.py:27
  575.1 2.4 fusion.87
  577.5 47.8 %fusion.69 = bf16[256,4,512]{2,1,0:T(4,128)(2,1)S(1)} fusion(bf16[256,512,576]{1,2,0:T(8,128)(2,1)} %get-tuple-element.11, f32[256,4,512]{2,1,0:T(4,128)} %get-tuple-element.20, f32[256,4]{1,0:T(8,128)S(1)} %get-tuple-element.19), kind=kOutput, calls=%fused_computation.71 | convolution fusion | flops 538443776 | bytes 137367552 | tf_op jit(solution)/shard_map/bht,btk->bhk/dot_general | solution.py:29
  625.3 0.3 copy.22
  625.6 7.1 fusion.12
  632.7 73.6 %all-reduce.6 = bf16[256,2048]{1,0:T(8,128)(2,1)S(1)} all-reduce(f32[256,2048]{1,0:T(8,128)} %fusion.12), channel_id=1, replica_groups=mesh['tp'=4,'dp'=2] {'tp'}, use_global_device_ids=true, to_apply=%region_10.11 | all-reduce | flops 524288 | bytes 3145728 | tf_op jit(solution)/shard_map/psum | solution.py:31
  706.2 0.0 copy-done.3
  706.2 0.5 fusion.63
  706.8 1.3 fusion.65
  708.1 0.0 all-gather.5.cloned.1.call-update
  708.1 0.0 reduce-scatter.5.cloned.1.call-start
  708.1 8.3 all-gather.5.cloned.1.call-done
  716.4 8.4 %fusion.22 = f32[512,1408]{1,0:T(8,128)} fusion(bf16[512,2048]{1,0:T(8,128)(2,1)} %all-gather.5.cloned.1.call-done, bf16[2,2048,1408]{2,1,0:T(8,128)(2,1)} %param.18), kind=kOutput, calls=%fused_computation.24 | convolution fusion | flops 2952790016 | bytes 10747904 | tf_op jit(solution)/shard_map/dot_general | solution.py:35
  724.8 0.0 copy-done.9
  724.8 13.8 %fusion.18 = f32[512,2048]{1,0:T(8,128)} fusion(bf16[2,1408,2048]{2,1,0:T(8,128)(2,1)} %param.19, bf16[512,2048]{1,0:T(8,128)(2,1)S(1)} %copy-done.9, bf16[2,2048,1408]{2,1,0:T(8,128)(2,1)} %param.17, f32[512,1408]{1,0:T(8,128)} %fusion.22), kind=kOutput, calls=%fused_computation.20 | convolution fusion | flops 5909905408 | bytes 20709376 | tf_op jit(solution)/shard_map/dot_general | solution.py:38
  738.6 0.0 reduce-scatter.5.cloned.1.call-update
  738.7 10.1 %reduce-scatter.5.cloned.1.call-done = f32[256,2048]{1,0:T(8,128)} async-done(((f32[512,2048]{1,0:T(8,128)}), f32[256,2048]{1,0:T(8,128)}) %reduce-scatter.5.cloned.1.call-update) | async-done | bytes 2097168 | tf_op jit(solution)/shard_map/reduce_scatter | solution.py:39
  748.7 77.1 %all-reduce.7 = bf16[256,2048]{1,0:T(8,128)(2,1)S(1)} all-reduce(f32[256,2048]{1,0:T(8,128)} %reduce-scatter.5.cloned.1.call-done), channel_id=1, replica_groups=mesh['tp'=4,'dp'=2] {'tp'}, use_global_device_ids=true, to_apply=%region_13.14 | all-reduce | flops 524288 | bytes 3145728 | tf_op jit(solution)/shard_map/psum | solution.py:40
  825.9 1.4 add.87
  (7 shorter events, 0.0 us)
Async XLA Ops:
  6.5 401.3 %all-gather.3.cloned.1.call-start = ((), (), s32[]{:S(2)}) async-start(), calls=%async_computation.2 | async-start | bytes 3145728 | tf_op jit(solution)/shard_map/all_gather | solution.py:34
  16.1 2.9 copy-start.7
  19.8 194.7 %copy-start = (bf16[256,4,576]{2,1,0:T(4,128)(2,1)S(1)}, bf16[256,4,576]{2,1,0:T(4,128)(2,1)}, u32[]{:S(2)}) copy-start(bf16[256,4,576]{2,1,0:T(4,128)(2,1)} %copy.14) | copy-start | bytes 3538948
  19.8 194.7 %copy-start.4 = (pred[256,512]{1,0:T(8,128)(4,1)S(1)}, pred[256,512]{1,0:T(8,128)(4,1)}, u32[]{:S(2)}) copy-start(pred[256,512]{1,0:T(8,128)(4,1)} %iota_compare_fusion) | copy-start | bytes 393220
  319.7 77.8 %copy-start.1 = (bf16[256,2048]{1,0:T(8,128)(2,1)S(1)}, bf16[256,2048]{1,0:T(8,128)(2,1)}, u32[]{:S(2)}) copy-start(bf16[256,2048]{1,0:T(8,128)(2,1)} %param.10) | copy-start | bytes 3145732
  397.5 0.7 copy-start.5
  399.6 40.6 %reduce-scatter.3.cloned.1.call-start = ((), (), s32[]{:S(2)}) async-start(), calls=%async_computation.3 | async-start | bytes 6291456 | tf_op jit(solution)/shard_map/reduce_scatter | solution.py:39
  407.8 8.4 %copy-start.8 = (bf16[512,2048]{1,0:T(8,128)(2,1)S(1)}, bf16[512,2048]{1,0:T(8,128)(2,1)}, u32[]{:S(2)}) copy-start(bf16[512,2048]{1,0:T(8,128)(2,1)} %all-gather.3.cloned.1.call-done) | copy-start | bytes 6291460
  430.1 286.3 %all-gather.5.cloned.1.call-start = ((), (), s32[]{:S(2)}) async-start(), calls=%async_computation.4 | async-start | bytes 3145728 | tf_op jit(solution)/shard_map/all_gather | solution.py:34
  517.5 1.5 copy-start.6
  518.0 1.0 copy-start.2
  632.7 73.6 %copy-start.3 = (bf16[256,2048]{1,0:T(8,128)(2,1)S(1)}, bf16[256,2048]{1,0:T(8,128)(2,1)}, u32[]{:S(2)}) copy-start(bf16[256,2048]{1,0:T(8,128)(2,1)} %copy-done.2) | copy-start | bytes 3145732
  708.1 40.7 %reduce-scatter.5.cloned.1.call-start = ((), (), s32[]{:S(2)}) async-start(), calls=%async_computation.5 | async-start | bytes 6291456 | tf_op jit(solution)/shard_map/reduce_scatter | solution.py:39
  716.4 8.4 %copy-start.9 = (bf16[512,2048]{1,0:T(8,128)(2,1)S(1)}, bf16[512,2048]{1,0:T(8,128)(2,1)}, u32[]{:S(2)}) copy-start(bf16[512,2048]{1,0:T(8,128)(2,1)} %all-gather.5.cloned.1.call-done) | copy-start | bytes 6291460
Sparse Core Ops, SparseCore 0:
  399.7 8.1 all-gather.2
  430.2 9.9 reduce-scatter.2
  708.2 8.1 all-gather.4
  738.8 9.9 reduce-scatter.4
where the time goes:
time: 843 us; the launch traced here: 834 us
  blocking collectives  306 us (36%)
  matrix products  263 us (31%)
  local copies, waits for them, and re-layouts  201 us (24%)
  waiting for transfers between devices  36.7 us (4%)
  other arithmetic  13.8 us (2%)
  between operations  13.8 us (2%)
    squeeze x1, local copies, waits for them, and re-layouts, body(): c = cache[l]  195 us
    psum x2, blocking collectives, body(): y = lax.psum(y, 'tp')  154 us
    psum x2, blocking collectives, body(): attn = lax.psum(jnp.dot(o, wo[l], preferred_element_type=jnp.float32), 'tp')  151 us
    dot_general x2, matrix products, body(): jnp.einsum('bht,btk->bhk', p, c[:, :, :LAT], preferred_element_type=jnp.f...  95.6 us
    dot_general x2, matrix products, body(): jnp.einsum('bhk,btk->bht', q, c, preferred_element_type=jnp.float32) * SCALE  95.4 us
    dot_general x2, matrix products, body(): yp = jnp.dot(a, w2[l], preferred_element_type=jnp.float32)  27.6 us
    reduce_scatter x2, waiting for transfers between devices, body(): y = lax.psum_scatter(yp, 'dp', scatter_dimension=0, tiled=True)  20.1 us
  transfers between devices with their start and end apart: 4, of which 4 were waited for; matrix products, arithmetic and copies ran while one was open for 0% of the time, Pallas kernels for 0%

commit v1 on v0

v1 whole, which is shorter than its diff:
```python
import functools

import jax
import jax.numpy as jnp
from jax import lax
from jax.experimental import pallas as pl
from jax.experimental.pallas import tpu as pltpu
from jax.sharding import PartitionSpec as P

LAT = 512
EPS = 1e-6
SCALE = 192 ** -0.5
MIB = 1024 * 1024


def _rmsnorm(v, w):
    vf = v.astype(jnp.float32)
    r = lax.rsqrt(jnp.mean(vf * vf, axis=-1, keepdims=True) + EPS)
    return (vf * r * w.astype(jnp.float32)).astype(jnp.bfloat16)


GROUP = 4
SLOTS = 3


def _attn_kernel(layer, rows, n_tp, lengths, q_ref, cache, o_ref, qf, of, buf, sem):
    hg, nb, cols = q_ref.shape
    s_len, kv = cache.shape[2], cache.shape[3]
    hpg = cols // kv
    nh = hg * hpg
    first = lax.axis_index('tp') * rows
    n_groups = rows // GROUP
    n_lane = qf.shape[0]

    def copies(g, slot):
        out = []
        for i in range(GROUP):
            out.append(pltpu.make_async_copy(
                cache.at[layer, first + g * GROUP + i], buf.at[slot, i], sem.at[slot, i]))
        return out

    for g in range(SLOTS - 1):
        for c in copies(g, g):
            c.start()

    for i in range(hg):
        for j in range(hpg // 2):
            pair = q_ref[i, :, 2 * kv * j:2 * kv * (j + 1)].astype(jnp.float32)
            other = pltpu.roll(pair, kv, 1)
            for k, v in ((2 * j, pair), (2 * j + 1, other)):
                h = i * hpg + k
                for n in range(n_lane):
                    qf[n, h * rows:(h + 1) * rows, :] = v[:, n * 128:(n + 1) * 128]

    def step(g, carry):
        slot = lax.rem(g, SLOTS)
        nxt = g + SLOTS - 1

        @pl.when(nxt < n_groups)
        def _():
            for c in copies(nxt, lax.rem(nxt, SLOTS)):
                c.start()

        for c in copies(g, slot):
            c.wait()
        for i in range(GROUP):
            b = g * GROUP + i
            q = jnp.concatenate([qf[n, pl.ds(b, nh, stride=rows), :] for n in range(n_lane)], axis=1)
            q = q[:, :kv].astype(jnp.bfloat16)
            c = buf[slot, i]
            s = lax.dot_general(q, c, (((1,), (1,)), ((), ())), preferred_element_type=jnp.float32) * SCALE
            pos = lax.broadcasted_iota(jnp.int32, s.shape, 1)
            s = jnp.where(pos < lengths[b], s, -jnp.inf)
            e = jnp.exp(s - jnp.max(s, axis=1, keepdims=True))
            p = (e / jnp.sum(e, axis=1, keepdims=True)).astype(jnp.bfloat16)
            o = jnp.dot(p, c[:, :LAT], preferred_element_type=jnp.float32)
            for n in range(LAT // 128):
                of[n, pl.ds(b, nh, stride=rows), :] = o[:, n * 128:(n + 1) * 128]
        return carry

    lax.fori_loop(0, n_groups, step, 0)
    for h in range(nh):
        for n in range(LAT // 128):
            k = (h % hpg) * LAT + n * 128
            o_ref[h // hpg, :, k:k + 128] = of[n, h * rows:(h + 1) * rows, :].astype(jnp.bfloat16)


def _attention(layer, q4, cache, lengths):
    hg, rows, cols = q4.shape
    s_len, kv = cache.shape[2:]
    nh = hg * cols // kv
    lanes = -(-kv // 128)
    return pl.pallas_call(
        functools.partial(_attn_kernel, layer, rows, hg),
        out_shape=jax.ShapeDtypeStruct((hg, rows, nh // hg * LAT), jnp.bfloat16),
        in_specs=[
            pl.BlockSpec(memory_space=pltpu.SMEM),
            pl.BlockSpec(memory_space=pltpu.VMEM),
            pl.BlockSpec(memory_space=pl.ANY),
        ],
        out_specs=pl.BlockSpec(memory_space=pltpu.VMEM),
        scratch_shapes=[
            pltpu.VMEM((lanes, nh * rows, 128), jnp.float32),
            pltpu.VMEM((LAT // 128, nh * rows, 128), jnp.float32),
            pltpu.VMEM((SLOTS, GROUP, s_len, kv), jnp.bfloat16),
            pltpu.SemaphoreType.DMA((SLOTS, GROUP)),
        ],
        compiler_params=pltpu.CompilerParams(vmem_limit_bytes=40 * MIB),
        cost_estimate=pl.CostEstimate(
            flops=4 * rows * nh * s_len * kv, bytes_accessed=rows * s_len * kv * 2, transcendentals=rows * nh * s_len),
        name=f'attention{layer}',
    )(lengths, q4, cache)


def solution(mesh):
    n_tp = mesh.shape['tp']

    def body(x, lengths, cache, attn_norm, ffn_norm, wq, wo, w1, w3, w2):
        nb, d = x.shape
        rows = nb // n_tp
        n_layers = cache.shape[0]
        me = lax.axis_index('tp')
        mine = lax.dynamic_slice_in_dim(lengths, me * rows, rows)
        xo = lax.dynamic_slice_in_dim(x, me * rows, rows)
        h = _rmsnorm(x, attn_norm[0])
        for l in range(n_layers):
            q = jnp.dot(h, wq[l], preferred_element_type=jnp.float32).astype(jnp.bfloat16)
            q4 = lax.all_to_all(q.reshape(n_tp, rows, -1), 'tp', 0, 0)
            o4 = _attention(l, q4, cache, mine)
            o = lax.all_to_all(o4, 'tp', 0, 0).reshape(nb, -1)
            attn = lax.psum_scatter(
                jnp.dot(o, wo[l], preferred_element_type=jnp.float32), 'tp', scatter_dimension=0, tiled=True)
            xo = xo + attn.astype(jnp.bfloat16)
            g = _rmsnorm(xo, ffn_norm[l])
            gg = lax.all_gather(g, ('dp', 'tp'), axis=0, tiled=True)
            u = jnp.dot(gg, w3[l], preferred_element_type=jnp.float32)
            v = jnp.dot(gg, w1[l], preferred_element_type=jnp.float32)
            a = (jax.nn.silu(u) * v).astype(jnp.bfloat16)
            yp = jnp.dot(a, w2[l], preferred_element_type=jnp.float32)
            y = lax.psum_scatter(yp, ('dp', 'tp'), scatter_dimension=0, tiled=True)
            xo = xo + y.astype(jnp.bfloat16)
            if l + 1 < n_layers:
                h = lax.all_gather(_rmsnorm(xo, attn_norm[l + 1]), 'tp', axis=0, tiled=True)
        return lax.all_gather(xo, 'tp', axis=0, tiled=True)

    in_specs = (
        P('dp', None),
        P('dp'),
        P(None, 'dp', None, None),
        P(None, None),
        P(None, None),
        P(None, None, 'tp'),
        P(None, 'tp', None),
        P(None, None, ('dp', 'tp')),
        P(None, None, ('dp', 'tp')),
        P(None, ('dp', 'tp'), None),
    )
    return jax.shard_map(body, mesh=mesh, in_specs=in_specs, out_specs=P('dp', None), check_vma=False)
```

time: 843 us -> 864 us (1.025)
  blocking collectives: 306 us -> 51.5 us
  local copies, waits for them, and re-layouts: 201 us -> 399 us
  matrix products: 263 us -> 66.4 us
  waiting for transfers between devices: 36.7 us -> 228 us
  Pallas kernels: 0 us -> 77.5 us
    unnamed x22, local copies, waits for them, and re-layouts: 1.69 us -> 399 us
    psum x4 -> x0, blocking collectives: 306 us -> none  [the longest x2 154 us: body(): y = lax.psum(y, 'tp')]
    dot_general x6 -> x2, matrix products: 205 us -> 7.41 us  [body(): jnp.dot(o, wo[l], preferred_element_type=jnp.float32)]
    squeeze x1 -> x0, local copies, waits for them, and re-layouts: 195 us -> none  [body(): c = cache[l]]
    reduce_scatter x2 -> x4, waiting for transfers between devices: 20.1 us -> 143 us  [the longest x2 85.1 us: body(): y = lax.psum_scatter(yp, ('dp', 'tp'), scatter_dimension=0, tiled=True)]
    pallas_call x0 -> x2, Pallas kernels: none -> 77.5 us  [_attention(): pl.pallas_call(functools.partial(_attn_kernel, layer, rows, hg), out_shap...]
    all_gather x2 -> x4, waiting for transfers between devices: 16.5 us -> 85.5 us  [the longest x2 43.9 us: body(): gg = lax.all_gather(g, ('dp', 'tp'), axis=0, tiled=True)]
    all_to_all x0 -> x3, blocking collectives: none -> 51.5 us  [the longest x2 33.5 us: body(): o = lax.all_to_all(o4, 'tp', 0, 0).reshape(nb, -1)]
  transfers between devices with their start and end apart: 4 -> 9, of which waited for: 4 -> 8; matrix products, arithmetic and copies ran while one was open for 0% -> 46% of each run, Pallas kernels for 0% -> 0%
where the time goes in v1:
time: 864 us; the launch traced here: 853 us
  local copies, waits for them, and re-layouts  399 us (46%)
  waiting for transfers between devices  228 us (26%)
  Pallas kernels  77.5 us (9%)
  matrix products  66.4 us (8%)
  blocking collectives  51.5 us (6%)
  between operations  13.6 us (2%)
  other arithmetic  11 us (1%)
    unnamed x22, local copies, waits for them, and re-layouts  399 us
    reduce_scatter x2, waiting for transfers between devices, body(): y = lax.psum_scatter(yp, ('dp', 'tp'), scatter_dimension=0, tiled=True)  85.1 us
    pallas_call x2, Pallas kernels, _attention(): pl.pallas_call(functools.partial(_attn_kernel, layer, rows, hg), out_shap...  77.5 us
    reduce_scatter x2, waiting for transfers between devices, body(): lax.psum_scatter(jnp.dot(o, wo[l], preferred_element_type=jnp.float32), '...  57.7 us
    all_gather x2, waiting for transfers between devices, body(): gg = lax.all_gather(g, ('dp', 'tp'), axis=0, tiled=True)  43.9 us
    all_to_all x2, blocking collectives, body(): o = lax.all_to_all(o4, 'tp', 0, 0).reshape(nb, -1)  33.5 us
    dot_general x2, matrix products, body(): yp = jnp.dot(a, w2[l], preferred_element_type=jnp.float32)  27.7 us
    all_gather x1, waiting for transfers between devices, body(): return lax.all_gather(xo, 'tp', axis=0, tiled=True)  20.8 us
  transfers between devices with their start and end apart: 9, of which 8 were waited for; matrix products, arithmetic and copies ran while one was open for 46% of the time, Pallas kernels for 0%

profile of v1, /device:TPU:0, one launch (start us, length us, event | category | flops | bytes accessed | tf_op | source)
XLA Modules:
  0.0 853.4 jit_solution(17477400494797941848)
XLA Ops:
  6.5 1.5 fusion.48
  8.1 1.4 slice_convert_fusion.1
  9.4 7.7 fusion.30
  17.2 5.6 all-to-all-start
  22.7 0.0 reduce-scatter.5.cloned.1.call-start
  22.7 0.0 copy-start.5
  22.7 396.2 %copy.11.cache = bf16[2,256,512,576]{3,2,1,0:T(8,128)(2,1)} copy(bf16[2,256,512,576]{2,3,1,0:T(8,128)(2,1)} %param.12) | data formatting | bytes 603979776 | tf_op args[2]
  418.9 0.0 copy-done.5
  418.9 0.1 dynamic_slice.7.lengths
  419.0 0.0 all-to-all-done.q_ref
  419.0 0.0 copy-start.2
  419.0 39.2 %attention0.1 = bf16[4,64,2048]{2,1,0:T(8,128)(2,1)S(1)} custom-call(s32[64]{0:T(128)S(1)} %dynamic_slice.7.lengths, bf16[4,64,2304]{2,1,0:T(8,128)(2,1)} %all-to-all-done.q_ref, bf16[2,256,512,576]{3,2,1,0:T(8,128)(2,1)} %copy.11.cache), custom_call_target="tpu_custom_call" | custom-call | flops 1207959552 | bytes 37748736 | tf_op jit(solution)/shard_map/attention0/pallas_call | solution.py:93
  458.2 18.3 %all_to_all.20 = bf16[4,64,2048]{2,1,0:T(8,128)(2,1)S(1)} all-to-all(bf16[4,64,2048]{2,1,0:T(8,128)(2,1)S(1)} %attention0.1), channel_id=1, replica_groups=mesh['tp'=4,'dp'=2] {'tp'}, dimensions={0} | all-to-all | bytes 2097152 | tf_op jit(solution)/shard_map/all_to_all | solution.py:130
  476.5 0.0 copy-done.2
  476.5 0.0 copy-start.1
  476.5 3.7 fusion.8
  480.2 0.0 reduce-scatter.5.cloned.1.call-update
  480.2 0.0 all-gather.5.cloned.1.call-start
  480.3 0.0 copy-done.1
  480.3 29.0 %reduce-scatter.5.cloned.1.call-done = f32[64,2048]{1,0:T(8,128)} async-done(((f32[256,2048]{1,0:T(8,128)}), f32[64,2048]{1,0:T(8,128)}) %reduce-scatter.5.cloned.1.call-update) | async-done | bytes 524304 | tf_op jit(solution)/shard_map/reduce_scatter | solution.py:131
  509.2 1.3 fusion.58
  510.6 0.8 fusion.60
  511.4 0.0 all-gather.5.cloned.1.call-update
  511.4 0.2 reduce-scatter.7.cloned.1.call-start
  511.7 21.9 %all-gather.5.cloned.1.call-done = bf16[512,2048]{1,0:T(8,128)(2,1)} async-done(((bf16[64,2048]{1,0:T(8,128)(2,1)}), bf16[512,2048]{1,0:T(8,128)(2,1)}) %all-gather.5.cloned.1.call-update) | async-done | bytes 2097168 | tf_op jit(solution)/shard_map/all_gather | solution.py:135
  533.5 8.4 fusion.22
  541.9 0.0 copy-done.3
  541.9 13.9 %fusion.18 = f32[512,2048]{1,0:T(8,128)} fusion(bf16[2,1408,2048]{2,1,0:T(8,128)(2,1)} %param.19, bf16[512,2048]{1,0:T(8,128)(2,1)S(1)} %copy-done.3, bf16[2,2048,1408]{2,1,0:T(8,128)(2,1)} %param.17, f32[512,1408]{1,0:T(8,128)} %fusion.22), kind=kOutput, calls=%fused_computation.18 | convolution fusion | flops 5909905408 | bytes 20709376 | tf_op jit(solution)/shard_map/dot_general | solution.py:139
  555.8 0.0 reduce-scatter.7.cloned.1.call-update
  555.8 0.0 all-gather.7.cloned.1.call-start
  555.9 42.5 %reduce-scatter.7.cloned.1.call-done = f32[64,2048]{1,0:T(8,128)} async-done(((f32[512,2048]{1,0:T(8,128)}), f32[64,2048]{1,0:T(8,128)}) %reduce-scatter.7.cloned.1.call-update) | async-done | bytes 524304 | tf_op jit(solution)/shard_map/reduce_scatter | solution.py:140
  598.4 1.2 fusion.61
  599.7 0.0 copy-done
  599.7 0.8 fusion.63
  600.5 0.0 all-gather.7.cloned.1.call-update
  600.5 0.0 reduce-scatter.9.cloned.1.call-start
  600.6 20.8 %all-gather.7.cloned.1.call-done = bf16[256,2048]{1,0:T(8,128)(2,1)} async-done(((bf16[64,2048]{1,0:T(8,128)(2,1)}), bf16[256,2048]{1,0:T(8,128)(2,1)}) %all-gather.7.cloned.1.call-update) | async-done | bytes 1048592 | tf_op jit(solution)/shard_map/all_gather | solution.py:143
  621.4 6.7 fusion.33
  628.1 18.0 %all_to_all.21.q_ref = bf16[4,64,2304]{2,1,0:T(8,128)(2,1)S(1)} all-to-all(bf16[4,64,2304]{2,1,0:T(8,128)(2,1)S(1)} %bitcast.61), channel_id=1, replica_groups=mesh['tp'=4,'dp'=2] {'tp'}, dimensions={0} | all-to-all | bytes 2359296 | tf_op jit(solution)/shard_map/all_to_all | solution.py:128
  646.1 38.3 %attention1.1 = bf16[4,64,2048]{2,1,0:T(8,128)(2,1)S(1)} custom-call(s32[64]{0:T(128)S(1)} %dynamic_slice.7.lengths, bf16[4,64,2304]{2,1,0:T(8,128)(2,1)S(1)} %all_to_all.21.q_ref, bf16[2,256,512,576]{3,2,1,0:T(8,128)(2,1)} %copy.11.cache), custom_call_target="tpu_custom_call" | custom-call | flops 1207959552 | bytes 37748736 | tf_op jit(solution)/shard_map/attention1/pallas_call | solution.py:93
  684.4 15.3 %all_to_all.22 = bf16[4,64,2048]{2,1,0:T(8,128)(2,1)S(1)} all-to-all(bf16[4,64,2048]{2,1,0:T(8,128)(2,1)S(1)} %attention1.1), channel_id=1, replica_groups=mesh['tp'=4,'dp'=2] {'tp'}, dimensions={0} | all-to-all | bytes 2097152 | tf_op jit(solution)/shard_map/all_to_all | solution.py:130
  699.7 0.0 slice-done
  699.7 0.0 slice-done.1
  699.7 0.0 slice-done.2
  699.7 0.0 slice-done.3
  699.7 3.7 fusion.6
  703.4 0.0 reduce-scatter.9.cloned.1.call-update
  703.5 0.3 all-gather.9.cloned.1.call-start
  703.7 28.8 %reduce-scatter.9.cloned.1.call-done = f32[64,2048]{1,0:T(8,128)} async-done(((f32[256,2048]{1,0:T(8,128)}), f32[64,2048]{1,0:T(8,128)}) %reduce-scatter.9.cloned.1.call-update) | async-done | bytes 524304 | tf_op jit(solution)/shard_map/reduce_scatter | solution.py:131
  732.5 1.2 fusion.64
  733.7 0.8 fusion.66
  734.6 0.0 all-gather.9.cloned.1.call-update
  734.6 0.0 reduce-scatter.11.cloned.1.call-start
  734.7 22.1 %all-gather.9.cloned.1.call-done = bf16[512,2048]{1,0:T(8,128)(2,1)} async-done(((bf16[64,2048]{1,0:T(8,128)(2,1)}), bf16[512,2048]{1,0:T(8,128)(2,1)}) %all-gather.9.cloned.1.call-update) | async-done | bytes 2097168 | tf_op jit(solution)/shard_map/all_gather | solution.py:135
  756.7 8.4 fusion.16
  765.1 0.0 copy-done.4
  765.1 13.8 %fusion.12 = f32[512,2048]{1,0:T(8,128)} fusion(bf16[2,1408,2048]{2,1,0:T(8,128)(2,1)} %param.19, bf16[512,2048]{1,0:T(8,128)(2,1)S(1)} %copy-done.4, bf16[2,2048,1408]{2,1,0:T(8,128)(2,1)} %param.17, f32[512,1408]{1,0:T(8,128)} %fusion.16), kind=kOutput, calls=%fused_computation.12 | convolution fusion | flops 5909905408 | bytes 20709376 | tf_op jit(solution)/shard_map/dot_general | solution.py:139
  779.0 0.0 reduce-scatter.11.cloned.1.call-update
  779.0 0.0 all-gather.11.cloned.1.call-start
  779.1 42.5 %reduce-scatter.11.cloned.1.call-done = f32[64,2048]{1,0:T(8,128)} async-done(((f32[512,2048]{1,0:T(8,128)}), f32[64,2048]{1,0:T(8,128)}) %reduce-scatter.11.cloned.1.call-update) | async-done | bytes 524304 | tf_op jit(solution)/shard_map/reduce_scatter | solution.py:140
  821.6 1.8 convert_add_fusion
  823.4 0.0 all-gather.11.cloned.1.call-update
  823.4 20.8 %all-gather.11.cloned.1.call-done = bf16[256,2048]{1,0:T(8,128)(2,1)} async-done(((bf16[64,2048]{1,0:T(8,128)(2,1)}), bf16[256,2048]{1,0:T(8,128)(2,1)}) %all-gather.11.cloned.1.call-update) | async-done | bytes 1048592 | tf_op jit(solution)/shard_map/all_gather | solution.py:144
  844.2 2.3 copy.14
  (13 shorter events, 0.1 us)
Async XLA Ops:
  17.2 401.9 %all-to-all-start = ((bf16[4,64,2304]{2,1,0:T(8,128)(2,1)}), bf16[4,64,2304]{2,1,0:T(8,128)(2,1)}, u32[]{:S(2)}, u32[]{:S(2)}) async-start(bf16[4,64,2304]{2,1,0:T(8,128)(2,1)} %bitcast.2), calls=%async_computation | async-start | bytes 2359296 | tf_op jit(solution)/shard_map/all_to_all | solution.py:128
  22.7 486.5 %reduce-scatter.5.cloned.1.call-start = ((), (), s32[]{:S(2)}) async-start(), calls=%async_computation.8 | async-start | bytes 2621440 | tf_op jit(solution)/shard_map/reduce_scatter | solution.py:131
  22.7 396.2 %copy-start.5 = (s32[256]{0:T(256)S(1)}, s32[256]{0:T(256)}, u32[]{:S(2)}) copy-start(s32[256]{0:T(256)} %param.11) | copy-start | bytes 3076
  419.0 57.5 %copy-start.2 = (bf16[2,2048,2048]{2,1,0:T(8,128)(2,1)S(1)}, bf16[2,2048,2048]{2,1,0:T(8,128)(2,1)}, u32[]{:S(2)}) copy-start(bf16[2,2048,2048]{2,1,0:T(8,128)(2,1)} %param.16) | copy-start | bytes 50331652
  476.5 3.8 copy-start.1
  480.2 53.3 %all-gather.5.cloned.1.call-start = ((), (), s32[]{:S(2)}) async-start(), calls=%async_computation.9 | async-start | bytes 2359296 | tf_op jit(solution)/shard_map/all_gather | solution.py:135
  511.4 87.0 %reduce-scatter.7.cloned.1.call-start = ((), (), s32[]{:S(2)}) async-start(), calls=%async_computation.10 | async-start | bytes 4718592 | tf_op jit(solution)/shard_map/reduce_scatter | solution.py:140
  533.5 8.4 copy-start.3
  555.8 43.9 %copy-start = (f32[1,2048]{1,0:T(1,128)S(1)}, f32[1,2048]{1,0:T(1,128)}, u32[]{:S(2)}) copy-start(f32[1,2048]{1,0:T(1,128)} %get-tuple-element.13) | copy-start | bytes 24580
  555.8 65.5 %all-gather.7.cloned.1.call-start = ((), (), s32[]{:S(2)}) async-start(), calls=%async_computation.11 | async-start | bytes 1310720 | tf_op jit(solution)/shard_map/all_gather | solution.py:143
  600.5 131.9 %reduce-scatter.9.cloned.1.call-start = ((), (), s32[]{:S(2)}) async-start(), calls=%async_computation.12 | async-start | bytes 2621440 | tf_op jit(solution)/shard_map/reduce_scatter | solution.py:131
  621.4 78.3 %slice-start = ((s8[16777216]{0:T(1024)(128)(4,1)}), s8[4194304]{0:T(1024)(128)(4,1)S(1)}, s32[]{:S(2)}) async-start(s8[16777216]{0:T(1024)(128)(4,1)} %bitcast.68), calls=%async_computation.16 | async-start | bytes 8388608
  646.1 53.6 %slice-start.1 = ((s8[16777216]{0:T(1024)(128)(4,1)}), s8[4194304]{0:T(1024)(128)(4,1)S(1)}, s32[]{:S(2)}) async-start(s8[16777216]{0:T(1024)(128)(4,1)} %bitcast.68), calls=%async_computation.17 | async-start | bytes 8388608
  646.1 53.6 %slice-start.2 = ((s8[16777216]{0:T(1024)(128)(4,1)}), s8[4194304]{0:T(1024)(128)(4,1)S(1)}, s32[]{:S(2)}) async-start(s8[16777216]{0:T(1024)(128)(4,1)} %bitcast.68), calls=%async_computation.18 | async-start | bytes 8388608
  646.1 53.6 %slice-start.3 = ((s8[16777216]{0:T(1024)(128)(4,1)}), s8[4194304]{0:T(1024)(128)(4,1)S(1)}, s32[]{:S(2)}) async-start(s8[16777216]{0:T(1024)(128)(4,1)} %bitcast.68), calls=%async_computation.19 | async-start | bytes 8388608
  703.5 53.3 %all-gather.9.cloned.1.call-start = ((), (), s32[]{:S(2)}) async-start(), calls=%async_computation.13 | async-start | bytes 2359296 | tf_op jit(solution)/shard_map/all_gather | solution.py:135
  734.6 87.0 %reduce-scatter.11.cloned.1.call-start = ((), (), s32[]{:S(2)}) async-start(), calls=%async_computation.14 | async-start | bytes 4718592 | tf_op jit(solution)/shard_map/reduce_scatter | solution.py:140
  756.7 8.4 copy-start.4
  779.0 65.2 %all-gather.11.cloned.1.call-start = ((), (), s32[]{:S(2)}) async-start(), calls=%async_computation.15 | async-start | bytes 1310720 | tf_op jit(solution)/shard_map/all_gather | solution.py:144
Sparse Core Ops, SparseCore 0:
  480.3 28.8 reduce-scatter.4
  511.5 21.9 all-gather.4
  556.0 42.4 reduce-scatter.6
  600.7 20.6 all-gather.6
  703.6 28.8 reduce-scatter.8
  734.7 21.9 all-gather.8
  779.1 42.4 reduce-scatter.10
  823.5 20.6 all-gather.10

commit v2 on v1

--- a/solution.py
+++ b/solution.py
@@ -25,7 +25,7 @@
 
 def _attn_kernel(layer, rows, n_tp, lengths, q_ref, cache, o_ref, qf, of, buf, sem):
     hg, nb, cols = q_ref.shape
-    s_len, kv = cache.shape[2], cache.shape[3]
+    kv = cache.shape[2]
     hpg = cols // kv
     nh = hg * hpg
     first = lax.axis_index('tp') * rows
@@ -68,12 +68,12 @@
             q = jnp.concatenate([qf[n, pl.ds(b, nh, stride=rows), :] for n in range(n_lane)], axis=1)
             q = q[:, :kv].astype(jnp.bfloat16)
             c = buf[slot, i]
-            s = lax.dot_general(q, c, (((1,), (1,)), ((), ())), preferred_element_type=jnp.float32) * SCALE
+            s = jnp.dot(q, c, preferred_element_type=jnp.float32) * SCALE
             pos = lax.broadcasted_iota(jnp.int32, s.shape, 1)
             s = jnp.where(pos < lengths[b], s, -jnp.inf)
             e = jnp.exp(s - jnp.max(s, axis=1, keepdims=True))
             p = (e / jnp.sum(e, axis=1, keepdims=True)).astype(jnp.bfloat16)
-            o = jnp.dot(p, c[:, :LAT], preferred_element_type=jnp.float32)
+            o = lax.dot_general(p, c[:LAT], (((1,), (1,)), ((), ())), preferred_element_type=jnp.float32)
             for n in range(LAT // 128):
                 of[n, pl.ds(b, nh, stride=rows), :] = o[:, n * 128:(n + 1) * 128]
         return carry
@@ -87,7 +87,7 @@
 
 def _attention(layer, q4, cache, lengths):
     hg, rows, cols = q4.shape
-    s_len, kv = cache.shape[2:]
+    kv, s_len = cache.shape[2:]
     nh = hg * cols // kv
     lanes = -(-kv // 128)
     return pl.pallas_call(
@@ -102,7 +102,7 @@
         scratch_shapes=[
             pltpu.VMEM((lanes, nh * rows, 128), jnp.float32),
             pltpu.VMEM((LAT // 128, nh * rows, 128), jnp.float32),
-            pltpu.VMEM((SLOTS, GROUP, s_len, kv), jnp.bfloat16),
+            pltpu.VMEM((SLOTS, GROUP, kv, s_len), jnp.bfloat16),
             pltpu.SemaphoreType.DMA((SLOTS, GROUP)),
         ],
         compiler_params=pltpu.CompilerParams(vmem_limit_bytes=40 * MIB),
@@ -119,6 +119,7 @@
         nb, d = x.shape
         rows = nb // n_tp
         n_layers = cache.shape[0]
+        cache = jnp.swapaxes(cache, 2, 3)
         me = lax.axis_index('tp')
         mine = lax.dynamic_slice_in_dim(lengths, me * rows, rows)
         xo = lax.dynamic_slice_in_dim(x, me * rows, rows)

time: 864 us -> 458 us (0.53); the launches traced: 853 us -> 458 us
  local copies, waits for them, and re-layouts: 399 us -> 2.41 us
  waiting for transfers between devices: 228 us -> 244 us
  Pallas kernels: 77.5 us -> 66 us
    unnamed x22 -> x19, local copies, waits for them, and re-layouts: 399 us -> 2.34 us
    all_to_all x1, waiting for transfers between devices: 0.01 us -> 14.7 us  [body(): q4 = lax.all_to_all(q.reshape(n_tp, rows, -1), 'tp', 0, 0)]
    pallas_call x2, Pallas kernels: 77.5 us -> 66 us  [_attention(): pl.pallas_call(functools.partial(_attn_kernel, layer, rows, hg), out_shap...]
  transfers between devices with their start and end apart: 9 -> 9, of which waited for: 8 -> 9; matrix products, arithmetic and copies ran while one was open for 46% -> 0% of each run, Pallas kernels for 0% -> 0%
where the time goes in v2:
time: 458 us
  waiting for transfers between devices  244 us (53%)
  matrix products  66.4 us (14%)
  Pallas kernels  66 us (14%)
  blocking collectives  49.3 us (11%)
  between operations  13.6 us (3%)
  other arithmetic  10.4 us (2%)
  starting transfers between devices  6.05 us (1%)
    reduce_scatter x2, waiting for transfers between devices, body(): y = lax.psum_scatter(yp, ('dp', 'tp'), scatter_dimension=0, tiled=True)  84.9 us
    pallas_call x2, Pallas kernels, _attention(): pl.pallas_call(functools.partial(_attn_kernel, layer, rows, hg), out_shap...  66 us
    reduce_scatter x2, waiting for transfers between devices, body(): lax.psum_scatter(jnp.dot(o, wo[l], preferred_element_type=jnp.float32), '...  58 us
    all_gather x2, waiting for transfers between devices, body(): gg = lax.all_gather(g, ('dp', 'tp'), axis=0, tiled=True)  44.1 us
    all_to_all x2, blocking collectives, body(): o = lax.all_to_all(o4, 'tp', 0, 0).reshape(nb, -1)  31.3 us
    dot_general x2, matrix products, body(): yp = jnp.dot(a, w2[l], preferred_element_type=jnp.float32)  27.7 us
    all_gather x1, waiting for transfers between devices, body(): return lax.all_gather(xo, 'tp', axis=0, tiled=True)  20.8 us
    all_gather x1, waiting for transfers between devices, body(): h = lax.all_gather(_rmsnorm(xo, attn_norm[l + 1]), 'tp', axis=0, tiled=True)  20.8 us
  transfers between devices with their start and end apart: 9, of which 9 were waited for; matrix products, arithmetic and copies ran while one was open for 0% of the time, Pallas kernels for 0%

profile of v2, /device:TPU:0, one launch (start us, length us, event | category | flops | bytes accessed | tf_op | source)
XLA Modules:
  0.0 457.7 jit_solution(16714779122679924370)
XLA Ops:
  6.5 1.5 fusion.48
  8.1 0.8 slice_convert_fusion.1
  8.9 0.0 copy-start.4
  8.9 7.7 %fusion.30 = bf16[256,2304]{1,0:T(8,128)(2,1)} fusion(bf16[2,2048,2304]{2,1,0:T(8,128)(2,1)} %param.15, bf16[256,2048]{1,0:T(8,128)(2,1)} %param.10, f32[2048]{0:T(1024)S(1)} %bitcast.68, f32[256]{0:T(256)S(1)} %add_rsqrt_fusion), kind=kOutput, calls=%fused_computation.30 | convolution fusion | flops 2418606080 | bytes 11674624 | tf_op jit(solution)/shard_map/dot_general | solution.py:128
  16.6 5.6 %all-to-all-start = ((bf16[4,64,2304]{2,1,0:T(8,128)(2,1)}), bf16[4,64,2304]{2,1,0:T(8,128)(2,1)S(1)}, u32[]{:S(2)}, u32[]{:S(2)}) async-start(bf16[4,64,2304]{2,1,0:T(8,128)(2,1)} %bitcast.2), calls=%async_computation | async-start | bytes 2359296 | tf_op jit(solution)/shard_map/all_to_all | solution.py:129
  22.2 0.0 reduce-scatter.5.cloned.1.call-start
  22.2 0.0 copy-done.4
  22.2 0.1 dynamic_slice.7.lengths
  22.2 14.7 %all-to-all-done.q_ref = bf16[4,64,2304]{2,1,0:T(8,128)(2,1)S(1)} async-done(((bf16[4,64,2304]{2,1,0:T(8,128)(2,1)}), bf16[4,64,2304]{2,1,0:T(8,128)(2,1)S(1)}, u32[]{:S(2)}, u32[]{:S(2)}) %all-to-all-start) | async-done | bytes 1179680 | tf_op jit(solution)/shard_map/all_to_all | solution.py:129
  37.0 0.0 copy-start.1
  37.0 33.0 %attention0.1 = bf16[4,64,2048]{2,1,0:T(8,128)(2,1)S(1)} custom-call(s32[64]{0:T(128)S(1)} %dynamic_slice.7.lengths, bf16[4,64,2304]{2,1,0:T(8,128)(2,1)S(1)} %all-to-all-done.q_ref, bf16[2,256,576,512]{3,2,1,0:T(8,128)(2,1)} %bitcast.3.cache), custom_call_target="tpu_custom_call" | custom-call | flops 1207959552 | bytes 37748736 | tf_op jit(solution)/shard_map/attention0/pallas_call | solution.py:93
  69.9 16.0 %all_to_all.20 = bf16[4,64,2048]{2,1,0:T(8,128)(2,1)S(1)} all-to-all(bf16[4,64,2048]{2,1,0:T(8,128)(2,1)S(1)} %attention0.1), channel_id=1, replica_groups=mesh['tp'=4,'dp'=2] {'tp'}, dimensions={0} | all-to-all | bytes 2097152 | tf_op jit(solution)/shard_map/all_to_all | solution.py:131
  86.0 0.0 copy-done.1
  86.0 0.0 copy-start
  86.0 3.7 fusion.8
  89.7 0.0 reduce-scatter.5.cloned.1.call-update
  89.7 0.0 all-gather.5.cloned.1.call-start
  89.8 0.0 copy-done
  89.8 29.0 %reduce-scatter.5.cloned.1.call-done = f32[64,2048]{1,0:T(8,128)} async-done(((f32[256,2048]{1,0:T(8,128)}), f32[64,2048]{1,0:T(8,128)}) %reduce-scatter.5.cloned.1.call-update) | async-done | bytes 524304 | tf_op jit(solution)/shard_map/reduce_scatter | solution.py:132
  118.8 1.3 fusion.58
  120.1 0.8 fusion.60
  121.0 0.0 all-gather.5.cloned.1.call-update
  121.0 0.0 reduce-scatter.7.cloned.1.call-start
  121.1 22.0 %all-gather.5.cloned.1.call-done = bf16[512,2048]{1,0:T(8,128)(2,1)} async-done(((bf16[64,2048]{1,0:T(8,128)(2,1)}), bf16[512,2048]{1,0:T(8,128)(2,1)}) %all-gather.5.cloned.1.call-update) | async-done | bytes 2097168 | tf_op jit(solution)/shard_map/all_gather | solution.py:136
  143.1 0.0 copy-start.2
  143.1 8.4 %fusion.22 = f32[512,1408]{1,0:T(8,128)} fusion(bf16[512,2048]{1,0:T(8,128)(2,1)} %all-gather.5.cloned.1.call-done, bf16[2,2048,1408]{2,1,0:T(8,128)(2,1)} %param.18), kind=kOutput, calls=%fused_computation.22 | convolution fusion | flops 2952790016 | bytes 10747904 | tf_op jit(solution)/shard_map/dot_general | solution.py:137
  151.5 0.0 copy-done.2
  151.5 13.8 %fusion.18 = f32[512,2048]{1,0:T(8,128)} fusion(bf16[2,1408,2048]{2,1,0:T(8,128)(2,1)} %param.19, bf16[512,2048]{1,0:T(8,128)(2,1)S(1)} %copy-done.2, bf16[2,2048,1408]{2,1,0:T(8,128)(2,1)} %param.17, f32[512,1408]{1,0:T(8,128)} %fusion.22), kind=kOutput, calls=%fused_computation.18 | convolution fusion | flops 5909905408 | bytes 20709376 | tf_op jit(solution)/shard_map/dot_general | solution.py:140
  165.4 0.0 reduce-scatter.7.cloned.1.call-update
  165.4 0.2 all-gather.7.cloned.1.call-start
  165.6 42.4 %reduce-scatter.7.cloned.1.call-done = f32[64,2048]{1,0:T(8,128)} async-done(((f32[512,2048]{1,0:T(8,128)}), f32[64,2048]{1,0:T(8,128)}) %reduce-scatter.7.cloned.1.call-update) | async-done | bytes 524304 | tf_op jit(solution)/shard_map/reduce_scatter | solution.py:141
  208.0 1.2 fusion.61
  209.3 0.8 fusion.63
  210.1 0.0 all-gather.7.cloned.1.call-update
  210.2 0.0 reduce-scatter.9.cloned.1.call-start
  210.2 20.8 %all-gather.7.cloned.1.call-done = bf16[256,2048]{1,0:T(8,128)(2,1)} async-done(((bf16[64,2048]{1,0:T(8,128)(2,1)}), bf16[256,2048]{1,0:T(8,128)(2,1)}) %all-gather.7.cloned.1.call-update) | async-done | bytes 1048592 | tf_op jit(solution)/shard_map/all_gather | solution.py:144
  231.0 0.0 slice-start
  231.0 6.7 %fusion.33 = bf16[256,2304]{1,0:T(8,128)(2,1)S(1)} fusion(bf16[256,2048]{1,0:T(8,128)(2,1)} %all-gather.7.cloned.1.call-done, bf16[2,2048,2304]{2,1,0:T(8,128)(2,1)} %param.15), kind=kOutput, calls=%fused_computation.31 | convolution fusion | flops 2416508928 | bytes 11665408 | tf_op jit(solution)/shard_map/dot_general | solution.py:128
  237.7 18.0 %all_to_all.21.q_ref = bf16[4,64,2304]{2,1,0:T(8,128)(2,1)S(1)} all-to-all(bf16[4,64,2304]{2,1,0:T(8,128)(2,1)S(1)} %bitcast.62), channel_id=1, replica_groups=mesh['tp'=4,'dp'=2] {'tp'}, dimensions={0} | all-to-all | bytes 2359296 | tf_op jit(solution)/shard_map/all_to_all | solution.py:129
  255.7 33.0 %attention1.1 = bf16[4,64,2048]{2,1,0:T(8,128)(2,1)S(1)} custom-call(s32[64]{0:T(128)S(1)} %dynamic_slice.7.lengths, bf16[4,64,2304]{2,1,0:T(8,128)(2,1)S(1)} %all_to_all.21.q_ref, bf16[2,256,576,512]{3,2,1,0:T(8,128)(2,1)} %bitcast.3.cache), custom_call_target="tpu_custom_call" | custom-call | flops 1207959552 | bytes 37748736 | tf_op jit(solution)/shard_map/attention1/pallas_call | solution.py:93
  288.8 15.2 %all_to_all.22 = bf16[4,64,2048]{2,1,0:T(8,128)(2,1)S(1)} all-to-all(bf16[4,64,2048]{2,1,0:T(8,128)(2,1)S(1)} %attention1.1), channel_id=1, replica_groups=mesh['tp'=4,'dp'=2] {'tp'}, dimensions={0} | all-to-all | bytes 2097152 | tf_op jit(solution)/shard_map/all_to_all | solution.py:131
  304.0 0.0 slice-done
  304.0 0.0 slice-done.1
  304.0 0.0 slice-done.2
  304.0 0.0 slice-done.3
  304.0 3.7 fusion.6
  307.7 0.0 reduce-scatter.9.cloned.1.call-update
  307.8 0.0 all-gather.9.cloned.1.call-start
  307.8 29.0 %reduce-scatter.9.cloned.1.call-done = f32[64,2048]{1,0:T(8,128)} async-done(((f32[256,2048]{1,0:T(8,128)}), f32[64,2048]{1,0:T(8,128)}) %reduce-scatter.9.cloned.1.call-update) | async-done | bytes 524304 | tf_op jit(solution)/shard_map/reduce_scatter | solution.py:132
  336.8 1.2 fusion.64
  338.0 0.8 fusion.66
  338.9 0.0 all-gather.9.cloned.1.call-update
  338.9 0.0 reduce-scatter.11.cloned.1.call-start
  339.0 22.1 %all-gather.9.cloned.1.call-done = bf16[512,2048]{1,0:T(8,128)(2,1)} async-done(((bf16[64,2048]{1,0:T(8,128)(2,1)}), bf16[512,2048]{1,0:T(8,128)(2,1)}) %all-gather.9.cloned.1.call-update) | async-done | bytes 2097168 | tf_op jit(solution)/shard_map/all_gather | solution.py:136
  361.0 8.4 %fusion.16 = f32[512,1408]{1,0:T(8,128)} fusion(bf16[512,2048]{1,0:T(8,128)(2,1)} %all-gather.9.cloned.1.call-done, bf16[2,2048,1408]{2,1,0:T(8,128)(2,1)} %param.18), kind=kOutput, calls=%fused_computation.16 | convolution fusion | flops 2952790016 | bytes 10747904 | tf_op jit(solution)/shard_map/dot_general | solution.py:137
  369.4 0.0 copy-done.3
  369.5 13.8 %fusion.12 = f32[512,2048]{1,0:T(8,128)} fusion(bf16[2,1408,2048]{2,1,0:T(8,128)(2,1)} %param.19, bf16[512,2048]{1,0:T(8,128)(2,1)S(1)} %copy-done.3, bf16[2,2048,1408]{2,1,0:T(8,128)(2,1)} %param.17, f32[512,1408]{1,0:T(8,128)} %fusion.16), kind=kOutput, calls=%fused_computation.12 | convolution fusion | flops 5909905408 | bytes 20709376 | tf_op jit(solution)/shard_map/dot_general | solution.py:140
  383.3 0.0 reduce-scatter.11.cloned.1.call-update
  383.3 0.0 all-gather.11.cloned.1.call-start
  383.4 42.5 %reduce-scatter.11.cloned.1.call-done = f32[64,2048]{1,0:T(8,128)} async-done(((f32[512,2048]{1,0:T(8,128)}), f32[64,2048]{1,0:T(8,128)}) %reduce-scatter.11.cloned.1.call-update) | async-done | bytes 524304 | tf_op jit(solution)/shard_map/reduce_scatter | solution.py:141
  425.9 1.8 convert_add_fusion
  427.7 0.0 all-gather.11.cloned.1.call-update
  427.7 20.8 %all-gather.11.cloned.1.call-done = bf16[256,2048]{1,0:T(8,128)(2,1)} async-done(((bf16[64,2048]{1,0:T(8,128)(2,1)}), bf16[256,2048]{1,0:T(8,128)(2,1)}) %all-gather.11.cloned.1.call-update) | async-done | bytes 1048592 | tf_op jit(solution)/shard_map/all_gather | solution.py:145
  448.6 2.3 copy.12
  (10 shorter events, 0.0 us)
Async XLA Ops:
  8.9 13.3 %copy-start.4 = (s32[256]{0:T(256)S(1)}, s32[256]{0:T(256)}, u32[]{:S(2)}) copy-start(s32[256]{0:T(256)} %param.11) | copy-start | bytes 3076
  16.6 20.4 %all-to-all-start = ((bf16[4,64,2304]{2,1,0:T(8,128)(2,1)}), bf16[4,64,2304]{2,1,0:T(8,128)(2,1)S(1)}, u32[]{:S(2)}, u32[]{:S(2)}) async-start(bf16[4,64,2304]{2,1,0:T(8,128)(2,1)} %bitcast.2), calls=%async_computation | async-start | bytes 2359296 | tf_op jit(solution)/shard_map/all_to_all | solution.py:129
  22.2 96.7 %reduce-scatter.5.cloned.1.call-start = ((), (), s32[]{:S(2)}) async-start(), calls=%async_computation.8 | async-start | bytes 2621440 | tf_op jit(solution)/shard_map/reduce_scatter | solution.py:132
  37.0 49.0 %copy-start.1 = (bf16[2,2048,2048]{2,1,0:T(8,128)(2,1)S(1)}, bf16[2,2048,2048]{2,1,0:T(8,128)(2,1)}, u32[]{:S(2)}) copy-start(bf16[2,2048,2048]{2,1,0:T(8,128)(2,1)} %param.16) | copy-start | bytes 50331652
  86.0 3.8 copy-start
  89.7 53.4 %all-gather.5.cloned.1.call-start = ((), (), s32[]{:S(2)}) async-start(), calls=%async_computation.9 | async-start | bytes 2359296 | tf_op jit(solution)/shard_map/all_gather | solution.py:136
  121.0 87.0 %reduce-scatter.7.cloned.1.call-start = ((), (), s32[]{:S(2)}) async-start(), calls=%async_computation.10 | async-start | bytes 4718592 | tf_op jit(solution)/shard_map/reduce_scatter | solution.py:141
  143.1 8.4 %copy-start.2 = (bf16[512,2048]{1,0:T(8,128)(2,1)S(1)}, bf16[512,2048]{1,0:T(8,128)(2,1)}, u32[]{:S(2)}) copy-start(bf16[512,2048]{1,0:T(8,128)(2,1)} %all-gather.5.cloned.1.call-done) | copy-start | bytes 6291460
  165.4 65.6 %all-gather.7.cloned.1.call-start = ((), (), s32[]{:S(2)}) async-start(), calls=%async_computation.11 | async-start | bytes 1310720 | tf_op jit(solution)/shard_map/all_gather | solution.py:144
  210.2 126.6 %reduce-scatter.9.cloned.1.call-start = ((), (), s32[]{:S(2)}) async-start(), calls=%async_computation.12 | async-start | bytes 2621440 | tf_op jit(solution)/shard_map/reduce_scatter | solution.py:132
  231.0 73.0 %slice-start = ((s8[16777216]{0:T(1024)(128)(4,1)}), s8[4194304]{0:T(1024)(128)(4,1)S(1)}, s32[]{:S(2)}) async-start(s8[16777216]{0:T(1024)(128)(4,1)} %bitcast.69), calls=%async_computation.16 | async-start | bytes 8388608
  255.7 48.3 %slice-start.1 = ((s8[16777216]{0:T(1024)(128)(4,1)}), s8[4194304]{0:T(1024)(128)(4,1)S(1)}, s32[]{:S(2)}) async-start(s8[16777216]{0:T(1024)(128)(4,1)} %bitcast.69), calls=%async_computation.17 | async-start | bytes 8388608
  255.7 48.3 %slice-start.2 = ((s8[16777216]{0:T(1024)(128)(4,1)}), s8[4194304]{0:T(1024)(128)(4,1)S(1)}, s32[]{:S(2)}) async-start(s8[16777216]{0:T(1024)(128)(4,1)} %bitcast.69), calls=%async_computation.18 | async-start | bytes 8388608
  255.7 48.3 %slice-start.3 = ((s8[16777216]{0:T(1024)(128)(4,1)}), s8[4194304]{0:T(1024)(128)(4,1)S(1)}, s32[]{:S(2)}) async-start(s8[16777216]{0:T(1024)(128)(4,1)} %bitcast.69), calls=%async_computation.19 | async-start | bytes 8388608
  307.8 53.3 %all-gather.9.cloned.1.call-start = ((), (), s32[]{:S(2)}) async-start(), calls=%async_computation.13 | async-start | bytes 2359296 | tf_op jit(solution)/shard_map/all_gather | solution.py:136
  338.9 87.0 %reduce-scatter.11.cloned.1.call-start = ((), (), s32[]{:S(2)}) async-start(), calls=%async_computation.14 | async-start | bytes 4718592 | tf_op jit(solution)/shard_map/reduce_scatter | solution.py:141
  361.0 8.4 %copy-start.3 = (bf16[512,2048]{1,0:T(8,128)(2,1)S(1)}, bf16[512,2048]{1,0:T(8,128)(2,1)}, u32[]{:S(2)}) copy-start(bf16[512,2048]{1,0:T(8,128)(2,1)} %all-gather.9.cloned.1.call-done) | copy-start | bytes 6291460
  383.3 65.2 %all-gather.11.cloned.1.call-start = ((), (), s32[]{:S(2)}) async-start(), calls=%async_computation.15 | async-start | bytes 1310720 | tf_op jit(solution)/shard_map/all_gather | solution.py:145
Sparse Core Ops, SparseCore 0:
  89.8 28.9 reduce-scatter.4
  121.1 21.9 all-gather.4
  165.5 42.4 reduce-scatter.6
  210.3 20.6 all-gather.6
  307.9 28.8 reduce-scatter.8
  339.0 21.9 all-gather.8
  383.4 42.4 reduce-scatter.10
  427.9 20.6 all-gather.10

commit v3 on v2

v3 whole, which is shorter than its diff:
```python
import functools

import jax
import jax.numpy as jnp
from jax import lax
from jax.experimental import pallas as pl
from jax.experimental.pallas import tpu as pltpu
from jax.sharding import PartitionSpec as P

LAT = 512
EPS = 1e-6
SCALE = 192 ** -0.5
MIB = 1024 * 1024
MESH = pl.DeviceIdType.MESH
BF, F32 = jnp.bfloat16, jnp.float32


def _rmsnorm(v, w):
    vf = v.astype(F32)
    r = lax.rsqrt(jnp.mean(vf * vf, axis=-1, keepdims=True) + EPS)
    return (vf * r * w.astype(F32)).astype(BF)


GROUP = 8
SLOTS = 3


def _attn_kernel(layer, rows, lengths, q_ref, cache, o_ref, qf, of, buf, sem):
    hg, nb, cols = q_ref.shape
    kv = cache.shape[2]
    hpg = cols // kv
    nh = hg * hpg
    first = lax.axis_index('tp') * rows
    n_groups = rows // GROUP
    n_lane = qf.shape[0]

    def copies(g, slot):
        return [pltpu.make_async_copy(cache.at[layer, first + g * GROUP + i], buf.at[slot, i], sem.at[slot, i])
                for i in range(GROUP)]

    for g in range(SLOTS - 1):
        for c in copies(g, g):
            c.start()

    for i in range(hg):
        for j in range(hpg // 2):
            pair = q_ref[i, :, 2 * kv * j:2 * kv * (j + 1)].astype(F32)
            other = pltpu.roll(pair, kv, 1)
            for k, v in ((2 * j, pair), (2 * j + 1, other)):
                h = i * hpg + k
                for n in range(n_lane):
                    qf[n, h * rows:(h + 1) * rows, :] = v[:, n * 128:(n + 1) * 128]

    def step(g, carry):
        slot = lax.rem(g, SLOTS)
        nxt = g + SLOTS - 1

        @pl.when(nxt < n_groups)
        def _():
            for c in copies(nxt, lax.rem(nxt, SLOTS)):
                c.start()

        for c in copies(g, slot):
            c.wait()
        ss, ps = [], []
        for i in range(GROUP):
            b = g * GROUP + i
            q = jnp.concatenate([qf[n, pl.ds(b, nh, stride=rows), :] for n in range(n_lane)], axis=1)
            q = q[:, :kv].astype(BF)
            ss.append(jnp.dot(q, buf[slot, i], preferred_element_type=F32) * SCALE)
        for i in range(GROUP):
            s = ss[i]
            pos = lax.broadcasted_iota(jnp.int32, s.shape, 1)
            s = jnp.where(pos < lengths[g * GROUP + i], s, -jnp.inf)
            e = jnp.exp(s - jnp.max(s, axis=1, keepdims=True))
            ps.append((e / jnp.sum(e, axis=1, keepdims=True)).astype(BF))
        for i in range(GROUP):
            o = lax.dot_general(ps[i], buf[slot, i, :LAT], (((1,), (1,)), ((), ())), preferred_element_type=F32)
            for n in range(LAT // 128):
                of[n, pl.ds(g * GROUP + i, nh, stride=rows), :] = o[:, n * 128:(n + 1) * 128]
        return carry

    lax.fori_loop(0, n_groups, step, 0)
    for h in range(nh):
        for n in range(LAT // 128):
            k = (h % hpg) * LAT + n * 128
            o_ref[h // hpg, :, k:k + 128] = of[n, h * rows:(h + 1) * rows, :].astype(BF)


def _attention(layer, q4, cache, lengths):
    hg, rows, cols = q4.shape
    kv, s_len = cache.shape[2:]
    nh = hg * cols // kv
    lanes = -(-kv // 128)
    return pl.pallas_call(
        functools.partial(_attn_kernel, layer, rows),
        out_shape=jax.ShapeDtypeStruct((hg, rows, nh // hg * LAT), BF),
        in_specs=[
            pl.BlockSpec(memory_space=pltpu.SMEM),
            pl.BlockSpec(memory_space=pltpu.VMEM),
            pl.BlockSpec(memory_space=pl.ANY),
        ],
        out_specs=pl.BlockSpec(memory_space=pltpu.VMEM),
        scratch_shapes=[
            pltpu.VMEM((lanes, nh * rows, 128), F32),
            pltpu.VMEM((LAT // 128, nh * rows, 128), F32),
            pltpu.VMEM((SLOTS, GROUP, kv, s_len), BF),
            pltpu.SemaphoreType.DMA((SLOTS, GROUP)),
        ],
        compiler_params=pltpu.CompilerParams(vmem_limit_bytes=50 * MIB),
        cost_estimate=pl.CostEstimate(
            flops=4 * rows * nh * s_len * kv, bytes_accessed=rows * s_len * kv * 2, transcendentals=rows * nh * s_len),
        name=f'attention{layer}',
    )(lengths, q4, cache)


def _remote(src, dst, ssem, rsem, dev):
    return pltpu.make_async_remote_copy(
        src_ref=src, dst_ref=dst, send_sem=ssem, recv_sem=rsem,
        device_id={'tp': dev[0], 'dp': dev[1]}, device_id_type=MESH)


def _places():
    tp, dp = lax.axis_index('tp'), lax.axis_index('dp')
    x, y = lax.rem(tp, 2), tp // 2
    chips = (tp, y * 2 + 1 - x, (1 - y) * 2 + x, (1 - y) * 2 + 1 - x)
    return chips, dp


def _barrier(devs):
    sem = pltpu.get_barrier_semaphore()
    for t, d in devs:
        pl.semaphore_signal(sem, inc=1, device_id={'tp': t, 'dp': d}, device_id_type=MESH)
    pl.semaphore_wait(sem, len(devs))


HOPS = (None, 1, 2)


class _Gather:
    def __init__(self, blk, to, chips, dp, ssem, rsem):
        self.blk, self.to, self.chips, self.dp, self.ssem, self.rsem = blk, to, chips, dp, ssem, rsem
        half = blk(0).shape[-1] // 2
        self.cut = [pl.ds(0, half), pl.ds(half, half)]

    def _hop(self, r, hop, half, k):
        return _remote(self.blk(r).at[:, self.cut[half]], self.to(r, hop).at[:, self.cut[half]],
                       self.ssem.at[k], self.rsem.at[k], (self.chips[hop], self.dp))

    def direct(self, hop, half):
        return self._hop(0, hop, half, (hop - 1) * 2 + half)

    def relay(self, hop):
        return self._hop(3 - hop, hop, 0 if hop == 2 else 1, 4 + hop - 1)

    def start(self):
        for hop, half in ((1, 0), (2, 1), (1, 1), (2, 0)):
            self.direct(hop, half).start()

    def near(self):
        self.direct(1, 0).wait_recv()
        self.relay(2).start()
        self.direct(2, 1).wait_recv()
        self.relay(1).start()

    def near_rest(self, hop):
        self.direct(hop, 1 if hop == 1 else 0).wait_recv()

    def far(self):
        self.relay(1).wait_recv()
        self.relay(2).wait_recv()

    def finish(self):
        for hop in (1, 2):
            self.direct(hop, 0).wait_send()
            self.direct(hop, 1).wait_send()
            self.relay(hop).wait_send()


CW = 256


def _scatter(sent, kept, s1, r1, kp, s2, r2, sem1s, sem1r, sem2s, sem2r, chips, dp, after=None):
    n = s1.shape[1]
    rows = s2.shape[2]

    def one(p, j):
        return _remote(s1.at[p, j], r1.at[p, j], sem1s.at[p, j], sem1r.at[p, j], (chips[1 + p], dp))

    def two(p, j):
        return _remote(s2.at[p, j], r2.at[p, j], sem2s.at[p, j], sem2r.at[p, j], (chips[2 - p], dp))

    def send(j, c):
        sent(j)
        for p in range(2):
            one(p, j).start()
        return c

    def forward(j, c):
        if after is None:
            kept(j)
        for p in range(2):
            one(p, j).wait_recv()
            s2[p, j] = kp[p, j, rows:] + r1[p, j, rows:]
            two(p, j).start()
        return c

    lax.fori_loop(0, n, send, 0)
    if after is not None:
        after()
    lax.fori_loop(0, n, forward, 0)

    def total(p, j):
        two(p, j).wait_recv()
        return kp[p, j, :rows] + r1[p, j, :rows] + r2[p, j]

    def finish():
        def fin(j, c):
            for p in range(2):
                one(p, j).wait_send()
                two(p, j).wait_send()
            return c
        lax.fori_loop(0, n, fin, 0)

    return total, finish


def _first_kernel(x_ref, norm, wq_h, q_out, wq, qs, wsem, ssem, rsem):
    chips, dp = _places()
    w = pltpu.make_async_copy(wq_h.at[0], wq, wsem)
    w.start()
    _barrier([(chips[r], dp) for r in (1, 2, 3)])
    w.wait()
    _q_blocks(lambda r: _rmsnorm(x_ref[chips[r]], norm[0:1, :]), (3, 1, 2, 0), chips, dp, wq, qs, q_out, ssem, rsem)


def _q_blocks(h_of, order, chips, dp, wq, qs, q_out, ssem, rsem):
    def send(r):
        return _remote(qs.at[r], q_out.at[chips[0]], ssem.at[r], rsem.at[r], (chips[r], dp))

    n = wq.shape[1] // CW
    for r in order:
        h = h_of(r)
        dst = qs.at[r] if r else q_out.at[chips[0]]

        def tile(t, c):
            cols = pl.ds(pl.multiple_of(t * CW, CW), CW)
            dst[:, cols] = jnp.dot(h, wq[:, cols], preferred_element_type=F32).astype(BF)
            return c

        lax.fori_loop(0, n, tile, 0)
        if r:
            send(r).start()
    for r in (1, 2, 3):
        send(r).wait_recv()
    for r in (1, 2, 3):
        send(r).wait_send()


def _layer_kernel(layer, last, o_ref, x_ref, fnorm, anorm, wo_h, w1_h, w3_h, w2_h, wq_h, *refs):
    if last:
        out, *refs = refs
    else:
        q_out, x_out, *refs = refs
    (wo, w1, w3, w2, wsem, ob, osem_s, osem_r,
     as1, ar1, akp, as2, ar2, asem, xs,
     g, gsem_s, gsem_r, dsem_s, dsem_r, act,
     lp, ds, dr, dds_s, dds_r, fs1, fr1, fkp, fs2, fr2, fsem, *refs) = refs
    chips, dp = _places()
    sib = (chips[0], 1 - dp)
    rows, d = x_ref.shape
    half = d // 2
    nch = half // CW

    srcs = [(wo_h, wo), (w3_h, w3), (w1_h, w1), (w2_h, w2)]
    if not last:
        wq, h_all, qs, hsem_s, hsem_r, qsem_s, qsem_r = refs
        srcs.append((wq_h, wq))
    else:
        hsem_s, hsem_r = refs
    loads = [pltpu.make_async_copy(s.at[layer + (s is wq_h)], v, wsem.at[i]) for i, (s, v) in enumerate(srcs)]
    for c in loads:
        c.start()
    _barrier([(chips[r], dp) for r in (1, 2, 3)] + [sib])

    def osend(r):
        return _remote(o_ref.at[chips[r]], ob.at[r], osem_s.at[r], osem_r.at[r], (chips[r], dp))

    for r in (3, 1, 2):
        osend(r).start()
    ob[0] = o_ref[chips[0]]
    for r in (1, 2, 3):
        osend(r).wait_recv()
    loads[0].wait()

    def cols(p, j):
        return pl.ds(pl.multiple_of(p * half + j * CW, CW), CW)

    def o_dot(a, b, p, j):
        lhs = jnp.concatenate([ob[a], ob[b]], axis=0)
        return jnp.dot(lhs, wo[:, cols(p, j)], preferred_element_type=F32)

    def sent(j):
        for p in range(2):
            as1[p, j] = o_dot(1 + p, 3, p, j)

    def kept(j):
        for p in range(2):
            akp[p, j] = o_dot(0, 2 - p, p, j)

    total, finish_a = _scatter(sent, kept, as1, ar1, akp, as2, ar2, asem.at[0], asem.at[1], asem.at[2], asem.at[3],
                               chips, dp)
    for p in range(2):
        for j in range(nch):
            c = slice(p * half + j * CW, p * half + (j + 1) * CW)
            xs[:, c] = x_ref[:, c] + total(p, j).astype(BF)

    g[0, 0] = _rmsnorm(xs[...], fnorm[layer:layer + 1, :])
    ag = _Gather(lambda r: g.at[r, 0], lambda r, hop: g.at[r ^ hop, 0], chips, dp, gsem_s, gsem_r)

    def cross(r):
        return _remote(g.at[r, 0], g.at[r, 1], dsem_s.at[r], dsem_r.at[r], sib)

    ag.start()
    cross(0).start()
    ag.near()
    ag.near_rest(1)
    cross(1).start()
    ag.near_rest(2)
    cross(2).start()
    for c in loads[1:3]:
        c.wait()
    for r in range(3):
        cross(r).wait_recv()

    f = w1.shape[1]
    full = f // CW

    def up(lo, hi, t0, t1, tail):
        m = (hi - lo) * 2 * rows

        def gate(u, v, cc, w):
            act[lo:hi, :, :, cc] = (jax.nn.silu(u) * v).astype(BF).reshape(hi - lo, 2, rows, w)

        def tile(t, c):
            cc = pl.ds(pl.multiple_of(t * CW, CW), CW)
            gg = g[lo:hi].reshape(m, d)
            u = jnp.dot(gg, w3[:, cc], preferred_element_type=F32)
            v = jnp.dot(gg, w1[:, cc], preferred_element_type=F32)
            gate(u, v, cc, CW)
            return c

        lax.fori_loop(t0, t1, tile, 0)
        if tail:
            gg = g[lo:hi].reshape(m, d)
            w = f - full * CW
            ww = jnp.concatenate([w3[:, full * CW:], w1[:, full * CW:]], axis=1)
            uv = jnp.dot(gg, ww, preferred_element_type=F32)
            gate(uv[:, :w], uv[:, w:], slice(full * CW, f), w)

    up(0, 3, 0, 3, False)
    ag.far()
    cross(3).start()
    up(0, 3, 3, full, True)
    cross(3).wait_recv()
    up(3, 4, 0, full, True)
    loads[3].wait()

    def dsend(k, p, j):
        return _remote(ds.at[k, p, j], dr.at[k, p, j], dds_s.at[k, p, j], dds_r.at[k, p, j], sib)

    def f_dot(k, j, c):
        for p in range(2):
            a, b = ((1 + p, 3), (0, 2 - p))[k]
            lhs = jnp.concatenate([act[a, 1], act[b, 1], act[a, 0], act[b, 0]], axis=0)
            res = jnp.dot(lhs, w2[:, cols(p, j)], preferred_element_type=F32)
            ds[k, p, j] = res[:2 * rows]
            dsend(k, p, j).start()
            lp[k, p, j] = res[2 * rows:]
        return c

    lax.fori_loop(0, nch, functools.partial(f_dot, 0), 0)

    def joined(k, dst, j):
        for p in range(2):
            dsend(k, p, j).wait_recv()
            dst[p, j] = lp[k, p, j] + dr[k, p, j]

    def after():
        lax.fori_loop(0, nch, functools.partial(f_dot, 1), 0)

        def join(j, c):
            joined(1, fkp, j)
            return c
        lax.fori_loop(0, nch, join, 0)

    total, finish_f = _scatter(functools.partial(joined, 0, fs1), None, fs1, fr1, fkp, fs2, fr2,
                               fsem.at[0], fsem.at[1], fsem.at[2], fsem.at[3], chips, dp, after)
    for p in range(2):
        for j in range(nch):
            c = slice(p * half + j * CW, p * half + (j + 1) * CW)
            xs[:, c] = xs[:, c] + total(p, j).astype(BF)

    if last:
        me = chips[0]
        out[me] = xs[...]
        hg = _Gather(lambda r: out.at[chips[r]], lambda r, hop: out.at[chips[r]], chips, dp, hsem_s, hsem_r)
        hg.start()
        hg.near()
        hg.near_rest(1)
        hg.near_rest(2)
        hg.far()
    else:
        x_out[...] = xs[...]
        h_all[0] = _rmsnorm(xs[...], anorm[layer + 1:layer + 2, :])
        hg = _Gather(lambda r: h_all.at[r], lambda r, hop: h_all.at[r ^ hop], chips, dp, hsem_s, hsem_r)
        hg.start()
        loads[4].wait()

        def h_of(r):
            if r == 1:
                hg.near()
            if r == 3:
                hg.far()
            elif r:
                hg.near_rest(r)
            return h_all[r]

        _q_blocks(h_of, (0, 1, 2, 3), chips, dp, wq, qs, q_out, qsem_s, qsem_r)

    for r in (1, 2, 3):
        osend(r).wait_send()
    finish_a()
    ag.finish()
    for r in range(4):
        cross(r).wait_send()

    def fin(j, c):
        for k in range(2):
            for p in range(2):
                dsend(k, p, j).wait_send()
        return c
    lax.fori_loop(0, nch, fin, 0)
    finish_f()
    hg.finish()


VM = pl.BlockSpec(memory_space=pltpu.VMEM)
HB = pl.BlockSpec(memory_space=pl.ANY)
DMA = pltpu.SemaphoreType.DMA


def _first(x, norm, wq):
    nb, d = x.shape
    rows = nb // 4
    qc = wq.shape[2]
    return pl.pallas_call(
        _first_kernel,
        out_shape=jax.ShapeDtypeStruct((4, rows, qc), BF),
        in_specs=[VM, VM, HB],
        out_specs=VM,
        scratch_shapes=[pltpu.VMEM((d, qc), BF), pltpu.VMEM((4, rows, qc), BF), DMA, DMA((4,)), DMA((4,))],
        compiler_params=pltpu.CompilerParams(collective_id=0, has_side_effects=True, vmem_limit_bytes=50 * MIB),
        name='first',
    )(x.reshape(4, rows, d), norm, wq)


def _layer(layer, last, o4, xo, fnorm, anorm, wo, w1, w3, w2, wq):
    rows, d = xo.shape
    ko = o4.shape[2]
    f = w1.shape[2]
    qc = wq.shape[2]
    nch = d // 2 // CW
    pair = lambda r: pltpu.VMEM((2, nch, r, CW), F32)
    quad = pltpu.VMEM((2, 2, nch, 2 * rows, CW), F32)
    scratch = [
        pltpu.VMEM((ko, d), BF), pltpu.VMEM((d, f), BF), pltpu.VMEM((d, f), BF), pltpu.VMEM((f, d), BF), DMA((5,)),
        pltpu.VMEM((4, rows, ko), BF), DMA((4,)), DMA((4,)),
        pair(2 * rows), pair(2 * rows), pair(2 * rows), pair(rows), pair(rows), DMA((4, 2, nch)),
        pltpu.VMEM((rows, d), BF),
        pltpu.VMEM((4, 2, rows, d), BF), DMA((6,)), DMA((6,)), DMA((4,)), DMA((4,)),
        pltpu.VMEM((4, 2, rows, f), BF),
        quad, quad, quad, DMA((2, 2, nch)), DMA((2, 2, nch)),
        pair(2 * rows), pair(2 * rows), pair(2 * rows), pair(rows), pair(rows), DMA((4, 2, nch)),
    ]
    if last:
        out_shape = jax.ShapeDtypeStruct((4, rows, d), BF)
        out_specs = VM
        scratch += [DMA((6,)), DMA((6,))]
    else:
        out_shape = (jax.ShapeDtypeStruct((4, rows, qc), BF), jax.ShapeDtypeStruct((rows, d), BF))
        out_specs = (VM, VM)
        scratch += [pltpu.VMEM((d, qc), BF), pltpu.VMEM((4, rows, d), BF), pltpu.VMEM((4, rows, qc), BF),
                    DMA((6,)), DMA((6,)), DMA((4,)), DMA((4,))]
    return pl.pallas_call(
        functools.partial(_layer_kernel, layer, last),
        out_shape=out_shape,
        in_specs=[VM, VM, VM, VM, HB, HB, HB, HB, HB],
        out_specs=out_specs,
        scratch_shapes=scratch,
        compiler_params=pltpu.CompilerParams(
            collective_id=1 + layer, has_side_effects=True, vmem_limit_bytes=63 * MIB),
        name=f'layer{layer}',
    )(o4, xo, fnorm, anorm, wo, w1, w3, w2, wq)


def solution(mesh):
    n_tp = mesh.shape['tp']

    def body(x, lengths, cache, attn_norm, ffn_norm, wq, wo, w1, w3, w2):
        nb, d = x.shape
        rows = nb // n_tp
        n_layers = cache.shape[0]
        cache = jnp.swapaxes(cache, 2, 3)
        me = lax.axis_index('tp')
        mine = lax.dynamic_slice_in_dim(lengths, me * rows, rows)
        xo = lax.dynamic_slice_in_dim(x, me * rows, rows)
        q4 = _first(x, attn_norm, wq)
        for l in range(n_layers):
            last = l + 1 == n_layers
            o4 = _attention(l, q4, cache, mine)
            res = _layer(l, last, o4, xo, ffn_norm, attn_norm, wo, w1, w3, w2, wq)
            if not last:
                q4, xo = res
        return res.reshape(nb, d)

    in_specs = (
        P('dp', None),
        P('dp'),
        P(None, 'dp', None, None),
        P(None, None),
        P(None, None),
        P(None, None, 'tp'),
        P(None, 'tp', None),
        P(None, None, ('dp', 'tp')),
        P(None, None, ('dp', 'tp')),
        P(None, ('dp', 'tp'), None),
    )
    return jax.shard_map(body, mesh=mesh, in_specs=in_specs, out_specs=P('dp', None), check_vma=False)
```

time: 458 us -> 266 us (0.58)
  waiting for transfers between devices: 244 us -> 0 us
  Pallas kernels: 66 us -> 255 us
  matrix products: 66.4 us -> 0 us
  blocking collectives: 49.3 us -> 0 us
  between operations: 13.6 us -> 0.07 us
  other arithmetic: 10.4 us -> 0 us
  local copies, waits for them, and re-layouts: 2.41 us -> 9.83 us
  starting transfers between devices: 6.05 us -> 0 us
    pallas_call x2 -> x5, Pallas kernels: 66 us -> 255 us  [the longest x2 192 us: _layer(): pl.pallas_call(functools.partial(_layer_kernel, layer, last), out_shape=o...]
    reduce_scatter x4 -> x0, waiting for transfers between devices: 143 us -> none  [the longest x2 84.9 us: body(): y = lax.psum_scatter(yp, ('dp', 'tp'), scatter_dimension=0, tiled=True)]
    all_gather x4 -> x0, waiting for transfers between devices: 85.7 us -> none  [the longest x2 44.1 us: body(): gg = lax.all_gather(g, ('dp', 'tp'), axis=0, tiled=True)]
    dot_general x8 -> x0, matrix products: 66.4 us -> none  [the longest x2 27.7 us: body(): yp = jnp.dot(a, w2[l], preferred_element_type=jnp.float32)]
    all_to_all x3 -> x0, blocking collectives: 49.3 us -> none  [the longest x2 31.3 us: body(): o = lax.all_to_all(o4, 'tp', 0, 0).reshape(nb, -1)]
    all_to_all x1 -> x0, waiting for transfers between devices: 14.7 us -> none  [body(): q4 = lax.all_to_all(q.reshape(n_tp, rows, -1), 'tp', 0, 0)]
    all_to_all x1 -> x0, starting transfers between devices: 5.58 us -> none  [body(): q4 = lax.all_to_all(q.reshape(n_tp, rows, -1), 'tp', 0, 0)]
    reduce_sum x4 -> x0, other arithmetic: 5.26 us -> none  [_rmsnorm(): r = lax.rsqrt(jnp.mean(vf * vf, axis=-1, keepdims=True) + EPS)]
  transfers between devices with their start and end apart: 9 -> 0, of which waited for: 9 -> 0; matrix products, arithmetic and copies ran while one was open for 0% -> 0% of each run, Pallas kernels for 0% -> 0%
where the time goes in v3:
time: 266 us; the launch traced here: 265 us
  Pallas kernels  255 us (96%)
  local copies, waits for them, and re-layouts  9.83 us (4%)
    pallas_call x2, Pallas kernels, _layer(): pl.pallas_call(functools.partial(_layer_kernel, layer, last), out_shape=o...  192 us
    pallas_call x2, Pallas kernels, _attention(): pl.pallas_call(functools.partial(_attn_kernel, layer, rows), out_shape=ja...  39 us
    pallas_call x1, Pallas kernels, _first(): pl.pallas_call(_first_kernel, out_shape=jax.ShapeDtypeStruct((4, rows, qc...  24.3 us
    unnamed x11, local copies, waits for them, and re-layouts  7.42 us

profile of v3, /device:TPU:0, one launch (start us, length us, event | category | flops | bytes accessed | tf_op | source)
XLA Modules:
  0.0 265.2 jit_solution(17604872308648150046)
XLA Ops:
  0.0 0.8 dynamic_slice.6.lengths
  0.8 1.7 constant_dynamic-slice_fusion.x_ref
  2.4 0.0 copy-start.2
  2.4 1.2 copy-done.2
  3.6 0.0 copy-start.4
  3.6 0.7 copy-done.4
  4.3 24.3 %first.1.q_ref = bf16[4,64,2304]{2,1,0:T(8,128)(2,1)S(1)} custom-call(bf16[4,64,2048]{2,1,0:T(8,128)(2,1)S(1)} %bitcast.3, bf16[2,2048]{1,0:T(2,128)(2,1)S(1)} %copy-done.4, bf16[2,2048,2304]{2,1,0:T(8,128)(2,1)} %wq_h.5), custom_call_target="tpu_custom_call" | custom-call | tf_op jit(solution)/shard_map/first/pallas_call | solution.py:457
  28.7 19.5 %attention0.1.o_ref = bf16[4,64,2048]{2,1,0:T(8,128)(2,1)S(1)} custom-call(s32[64]{0:T(128)S(1)} %dynamic_slice.6.lengths, bf16[4,64,2304]{2,1,0:T(8,128)(2,1)S(1)} %first.1.q_ref, bf16[2,256,576,512]{3,2,1,0:T(8,128)(2,1)} %bitcast.1.cache), custom_call_target="tpu_custom_call" | custom-call | flops 1207959552 | bytes 37748736 | tf_op jit(solution)/shard_map/attention0/pallas_call | solution.py:95
  48.2 0.0 copy-start
  48.2 1.0 copy-done
  49.2 105.5 %layer0.1 = (bf16[4,64,2304]{2,1,0:T(8,128)(2,1)}, bf16[64,2048]{1,0:T(8,128)(2,1)}) custom-call(bf16[4,64,2048]{2,1,0:T(8,128)(2,1)} %copy-done, bf16[64,2048]{1,0:T(8,128)(2,1)} %constant_dynamic-slice_fusion.x_ref, bf16[2,2048]{1,0:T(2,128)(2,1)} %fnorm.3, bf16[2,2048]{1,0:T(2,128)(2,1)} %anorm.3, bf16[2,2048,2048]{2,1,0:T(8,128)(2,1)} %wo_h.3, ...), custom_call_target="tpu_custom_call" | custom-call | tf_op jit(solution)/shard_map/layer0/pallas_call | solution.py:495
  154.6 0.0 copy-start.3
  154.6 1.3 copy-done.3
  155.9 19.5 %attention1.1.o_ref = bf16[4,64,2048]{2,1,0:T(8,128)(2,1)S(1)} custom-call(s32[64]{0:T(128)S(1)} %dynamic_slice.6.lengths, bf16[4,64,2304]{2,1,0:T(8,128)(2,1)S(1)} %copy-done.3, bf16[2,256,576,512]{3,2,1,0:T(8,128)(2,1)} %bitcast.1.cache), custom_call_target="tpu_custom_call" | custom-call | flops 1207959552 | bytes 37748736 | tf_op jit(solution)/shard_map/attention1/pallas_call | solution.py:95
  175.4 0.0 copy-start.1
  175.4 1.0 copy-done.1
  176.4 86.5 %layer1.1 = bf16[4,64,2048]{2,1,0:T(8,128)(2,1)} custom-call(bf16[4,64,2048]{2,1,0:T(8,128)(2,1)} %copy-done.1, bf16[64,2048]{1,0:T(8,128)(2,1)} %get-tuple-element.8.x_ref, bf16[2,2048]{1,0:T(2,128)(2,1)} %fnorm.3, bf16[2,2048]{1,0:T(2,128)(2,1)} %anorm.3, bf16[2,2048,2048]{2,1,0:T(8,128)(2,1)} %wo_h.3, bf16[2,2048,1408]{2,1,0:T(8,128)(2,1)} %w1_h.3, ...), custom_call_target="tpu_custom_call" | custom-call | tf_op jit(solution)/shard_map/layer1/pallas_call | solution.py:495
  262.9 2.3 copy.12
Async XLA Ops:
  2.4 1.2 copy-start.2
  3.6 0.7 copy-start.4
  48.2 1.0 copy-start
  154.6 1.3 copy-start.3
  175.4 1.0 copy-start.1
